TPU v7x, 256 devices: a whole 4x4x8 slice. The times are simulated.
256 devices in a mesh: row: 32 (over z_hi, x, core), col: 8 (over y, z_lo).
Axes of the slice: x: 4, y: 4, z: 8 (z_hi: 4, z_lo: 2; z = z_hi * 2 + z_lo), core: 2. Of those that a mesh axis runs over, the one named last changes fastest.
Arguments:
- pivots: int32 [256], replicated, may hold values from 0 to 32767, as said below
- panel: float32 [32768, 256], P(('row', 'col')), may hold values from -6 to 6
- prior: bfloat16 [32768, 3072], P(('row', 'col')), may hold values from -0.796875 to 0.796875
- finished: bfloat16 [32768, 256], P(('row', 'col')), may hold values from -6 to 6
- pairs: int32 [32768], replicated, may hold values from 0 to 639999, as said below
- occupied: bfloat16 [800, 120], replicated, may hold values from -0.21875 to 0.21875
Outputs:
- updated: float32 [32768, 256], P(('row', 'col'))
- halves: float32 [256, 120, 800], P(('row', 'col'))
Inputs may be any that keep to these rules, and one draw needn't show every extreme that they name: `pivots`: distinct rows; at most 2 of them lie among the rows of one device (aligned blocks of 128 rows), and one device holds exactly 2. `pairs`: each value a * 800 + b with 0 <= b <= a < 800; all distinct and increasing.
All inputs are finite; a program needn't handle non-finite values.
Results may differ from a plain program's by a relative error of at most 0.0003.
Values may be sent and summed in bfloat16 or wider, within the bound.
A program may use at most 64 MiB of HBM per device.

v0:
```python
import jax
import jax.numpy as jnp
from jax import lax
from jax.sharding import PartitionSpec as P


def half_transform(received, pair_ids, occupied):
    orbitals = occupied.shape[0]
    pair_count = received.shape[0]
    vector_count = received.shape[1]
    first_ao = pair_ids // orbitals
    second_ao = pair_ids % orbitals
    off_diag = first_ao != second_ao
    occ_first = jnp.take(occupied, first_ao, axis=0)
    occ_second = jnp.where(
        off_diag[:, None], jnp.take(occupied, second_ao, axis=0), jnp.zeros((), jnp.bfloat16)
    )
    coeffs = jnp.concatenate([occ_first, occ_second], axis=0)
    targets = jnp.concatenate([second_ao, first_ao], axis=0).astype(jnp.int32)
    entries = jnp.concatenate([received, received], axis=0)
    doubled = 2 * pair_count
    wanted = min(doubled, max(1024, doubled // 8))
    block_rows = wanted
    for candidate in range(wanted, 0, -1):
        if doubled % candidate == 0:
            block_rows = candidate
            break
    columns = jnp.arange(orbitals, dtype=jnp.int32)

    def one_block(block_index, accumulated):
        start = block_index * block_rows
        coeff_block = lax.dynamic_slice_in_dim(coeffs, start, block_rows, 0)
        target_block = lax.dynamic_slice_in_dim(targets, start, block_rows, 0)
        entry_block = lax.dynamic_slice_in_dim(entries, start, block_rows, 0)
        matches = target_block[:, None] == columns[None, :]
        spread = jnp.where(
            matches[None, :, :], entry_block.T[:, :, None], jnp.zeros((), jnp.bfloat16)
        )
        return accumulated + jnp.einsum(
            "pi,vpm->vim", coeff_block, spread, preferred_element_type=jnp.float32
        )

    initial = jnp.zeros((vector_count, occupied.shape[1], orbitals), jnp.float32)
    return lax.fori_loop(0, doubled // block_rows, one_block, initial)


def per_device(pivots, panel, prior, finished, pairs, occupied):
    rows_dev = prior.shape[0]
    row_count = lax.axis_size("row")
    col_count = lax.axis_size("col")
    own_index = lax.axis_index("row") * col_count + lax.axis_index("col")
    owner = pivots // rows_dev
    local_rows = pivots % rows_dev
    owned = owner == own_index
    picked = jnp.take(prior, local_rows, axis=0).astype(jnp.float32)
    contribution = jnp.where(owned[:, None], picked, jnp.zeros_like(picked))
    pivot_rows = lax.psum(contribution, ("row", "col")).astype(jnp.bfloat16)
    updated = panel - lax.dot_general(
        prior, pivot_rows, (((1,), (1,)), ((), ())), preferred_element_type=jnp.float32
    )
    by_device = pairs.reshape(row_count, col_count, rows_dev)
    col_pairs = lax.dynamic_slice_in_dim(by_device, lax.axis_index("col"), 1, 1).reshape(-1)
    grouped = finished.reshape(rows_dev, row_count, finished.shape[1] // row_count)
    received = lax.all_to_all(grouped, "row", split_axis=1, concat_axis=0, tiled=True)
    partials = half_transform(
        received.reshape(received.shape[0], received.shape[2]), col_pairs, occupied
    )
    halves = lax.psum_scatter(partials, "col", scatter_dimension=0, tiled=True)
    return (updated, halves)


def solution(mesh):
    return jax.shard_map(
        per_device,
        mesh=mesh,
        in_specs=(
            P(),
            P(("row", "col"), None),
            P(("row", "col"), None),
            P(("row", "col"), None),
            P(),
            P(),
        ),
        out_specs=(P(("row", "col"), None), P(("row", "col"), None, None)),
        check_vma=False,
    )
```

profile of v0, /device:TPU:32, one launch (start us, length us, event | category | flops | bytes accessed | tf_op | source)
XLA Modules:
  0.0 254.6 jit_solution(17810283203826027613)
XLA Ops:
  7.2 0.0 copy-start
  7.2 0.0 copy-start.1
  7.2 1.7 copy.17
  8.9 10.4 %all-to-all-start = ((bf16[128,32,8]{0,2,1:T(8,128)(2,1)}), bf16[128,32,8]{0,2,1:T(8,128)(2,1)S(1)}, u32[]{:S(2)}, u32[]{:S(2)}) async-start(bf16[128,32,8]{0,2,1:T(8,128)(2,1)} %bitcast.4), calls=%async_computation | async-start | bytes 131072 | tf_op jit(solution)/shard_map/all_to_all | solution.py:64
  19.3 0.0 reduce-scatter.2.cloned.1.call-start
  19.3 1.0 broadcast_remainder_fusion
  20.3 1.0 compare_reduce_fusion
  21.4 0.0 copy-done.1
  21.4 12.1 %gather_fusion.2 = bf16[4096,120]{1,0:T(8,128)(2,1)S(1)} fusion(bf16[800,120]{1,0:T(8,128)(2,1)S(1)} %copy-done.1, s32[4096]{0:T(1024)S(1)} %get-tuple-element.172), kind=kCustom, calls=%fused_computation.1.clone | custom fusion | bytes 1982464 | tf_op jit(solution)/shard_map/jit(_take)/gather | solution.py:16
  33.5 12.1 %gather_fusion.1 = bf16[4096,120]{1,0:T(8,128)(2,1)S(1)} fusion(bf16[800,120]{1,0:T(8,128)(2,1)S(1)} %copy-done.1, s32[4096]{0:T(1024)S(1)} %fusion.21), kind=kCustom, calls=%fused_computation.clone | custom fusion | bytes 1982464 | tf_op jit(solution)/shard_map/jit(_take)/gather | solution.py:14
  45.7 2.1 broadcast_select_fusion
  47.8 1.4 select_select_fusion
  49.2 0.4 pad_maximum_fusion
  49.7 3.0 %copy.18 = bf16[8192,120]{0,1:T(8,128)(2,1)} copy(bf16[8192,120]{1,0:T(8,128)(2,1)S(1)} %pad_maximum_fusion) | data formatting | bytes 3932160
  52.6 0.0 all-to-all-done
  52.7 55.6 %while.14 = (s32[]{:T(128)}, f32[8,120,800]{1,2,0:T(8,128)}, s32[8192]{0:T(1024)S(1)}, bf16[8192,8]{0,1:T(8,128)(2,1)S(1)}, bf16[8192,120]{0,1:T(8,128)(2,1)}, /*index=5*/s32[]{:T(128)}, s32[]{:T(128)}, s32[]{:T(128)}, s32[]{:T(128)}) while((s32[]{:T(128)}, f32[8,120,800]{1,2,0:T(8,128)}, s32[8192]{0:T(1024)S(1)}, ...), condition=%wide.region_2.4_spmd.clone, body=%wide.region_1.3_spmd.clone.sunk | while | flops 1581772800 | bytes 8294561 | solution.py:44
  52.7 0.6 iota_compare_fusion.2
  53.3 5.9 %bitcast_add_fusion.2 = f32[8,120,800]{1,2,0:T(8,128)} fusion(f32[8,120,800]{1,2,0:T(8,128)} %get-tuple-element.216, pred[1024,800]{0,1:T(8,128)(4,1)S(1)} %iota_compare_fusion.2, bf16[8,1024]{1,0:T(8,128)(2,1)S(1)} %dynamic-slice_bitcast_fusion.2, pred[]{:T(512)S(6)} %compare.6, bf16[8192,120]{0,1:T(8,128)(2,1)} %get-tuple-element.228, ...), kind=kOutput, calls=%fused_computation.9.clone.1 | convolution fusion | flops 1580953600 | bytes 7430149 | tf_op jit(solution)/shard_map/while/body/eval_jaxpr/pi,vpm->vim/dot_general | solution.py:39
  59.2 0.6 iota_compare_fusion.2
  59.9 6.4 %bitcast_add_fusion.2 = f32[8,120,800]{1,2,0:T(8,128)} fusion(f32[8,120,800]{1,2,0:T(8,128)} %get-tuple-element.216, pred[1024,800]{0,1:T(8,128)(4,1)S(1)} %iota_compare_fusion.2, bf16[8,1024]{1,0:T(8,128)(2,1)S(1)} %dynamic-slice_bitcast_fusion.2, pred[]{:T(512)S(6)} %compare.6, bf16[8192,120]{0,1:T(8,128)(2,1)} %get-tuple-element.228, ...), kind=kOutput, calls=%fused_computation.9.clone.1 | convolution fusion | flops 1580953600 | bytes 7430149 | tf_op jit(solution)/shard_map/while/body/eval_jaxpr/pi,vpm->vim/dot_general | solution.py:39
  66.2 0.6 iota_compare_fusion.2
  66.9 6.4 %bitcast_add_fusion.2 = f32[8,120,800]{1,2,0:T(8,128)} fusion(f32[8,120,800]{1,2,0:T(8,128)} %get-tuple-element.216, pred[1024,800]{0,1:T(8,128)(4,1)S(1)} %iota_compare_fusion.2, bf16[8,1024]{1,0:T(8,128)(2,1)S(1)} %dynamic-slice_bitcast_fusion.2, pred[]{:T(512)S(6)} %compare.6, bf16[8192,120]{0,1:T(8,128)(2,1)} %get-tuple-element.228, ...), kind=kOutput, calls=%fused_computation.9.clone.1 | convolution fusion | flops 1580953600 | bytes 7430149 | tf_op jit(solution)/shard_map/while/body/eval_jaxpr/pi,vpm->vim/dot_general | solution.py:39
  73.2 0.6 iota_compare_fusion.2
  73.9 6.4 %bitcast_add_fusion.2 = f32[8,120,800]{1,2,0:T(8,128)} fusion(f32[8,120,800]{1,2,0:T(8,128)} %get-tuple-element.216, pred[1024,800]{0,1:T(8,128)(4,1)S(1)} %iota_compare_fusion.2, bf16[8,1024]{1,0:T(8,128)(2,1)S(1)} %dynamic-slice_bitcast_fusion.2, pred[]{:T(512)S(6)} %compare.6, bf16[8192,120]{0,1:T(8,128)(2,1)} %get-tuple-element.228, ...), kind=kOutput, calls=%fused_computation.9.clone.1 | convolution fusion | flops 1580953600 | bytes 7430149 | tf_op jit(solution)/shard_map/while/body/eval_jaxpr/pi,vpm->vim/dot_general | solution.py:39
  80.3 0.6 iota_compare_fusion.2
  80.9 6.4 %bitcast_add_fusion.2 = f32[8,120,800]{1,2,0:T(8,128)} fusion(f32[8,120,800]{1,2,0:T(8,128)} %get-tuple-element.216, pred[1024,800]{0,1:T(8,128)(4,1)S(1)} %iota_compare_fusion.2, bf16[8,1024]{1,0:T(8,128)(2,1)S(1)} %dynamic-slice_bitcast_fusion.2, pred[]{:T(512)S(6)} %compare.6, bf16[8192,120]{0,1:T(8,128)(2,1)} %get-tuple-element.228, ...), kind=kOutput, calls=%fused_computation.9.clone.1 | convolution fusion | flops 1580953600 | bytes 7430149 | tf_op jit(solution)/shard_map/while/body/eval_jaxpr/pi,vpm->vim/dot_general | solution.py:39
  87.3 0.6 iota_compare_fusion.2
  87.9 6.4 %bitcast_add_fusion.2 = f32[8,120,800]{1,2,0:T(8,128)} fusion(f32[8,120,800]{1,2,0:T(8,128)} %get-tuple-element.216, pred[1024,800]{0,1:T(8,128)(4,1)S(1)} %iota_compare_fusion.2, bf16[8,1024]{1,0:T(8,128)(2,1)S(1)} %dynamic-slice_bitcast_fusion.2, pred[]{:T(512)S(6)} %compare.6, bf16[8192,120]{0,1:T(8,128)(2,1)} %get-tuple-element.228, ...), kind=kOutput, calls=%fused_computation.9.clone.1 | convolution fusion | flops 1580953600 | bytes 7430149 | tf_op jit(solution)/shard_map/while/body/eval_jaxpr/pi,vpm->vim/dot_general | solution.py:39
  94.3 0.6 iota_compare_fusion.2
  94.9 6.4 %bitcast_add_fusion.2 = f32[8,120,800]{1,2,0:T(8,128)} fusion(f32[8,120,800]{1,2,0:T(8,128)} %get-tuple-element.216, pred[1024,800]{0,1:T(8,128)(4,1)S(1)} %iota_compare_fusion.2, bf16[8,1024]{1,0:T(8,128)(2,1)S(1)} %dynamic-slice_bitcast_fusion.2, pred[]{:T(512)S(6)} %compare.6, bf16[8192,120]{0,1:T(8,128)(2,1)} %get-tuple-element.228, ...), kind=kOutput, calls=%fused_computation.9.clone.1 | convolution fusion | flops 1580953600 | bytes 7430149 | tf_op jit(solution)/shard_map/while/body/eval_jaxpr/pi,vpm->vim/dot_general | solution.py:39
  101.3 0.6 iota_compare_fusion.2
  101.9 6.4 %bitcast_add_fusion.2 = f32[8,120,800]{1,2,0:T(8,128)} fusion(f32[8,120,800]{1,2,0:T(8,128)} %get-tuple-element.216, pred[1024,800]{0,1:T(8,128)(4,1)S(1)} %iota_compare_fusion.2, bf16[8,1024]{1,0:T(8,128)(2,1)S(1)} %dynamic-slice_bitcast_fusion.2, pred[]{:T(512)S(6)} %compare.6, bf16[8192,120]{0,1:T(8,128)(2,1)} %get-tuple-element.228, ...), kind=kOutput, calls=%fused_computation.9.clone.1 | convolution fusion | flops 1580953600 | bytes 7430149 | tf_op jit(solution)/shard_map/while/body/eval_jaxpr/pi,vpm->vim/dot_general | solution.py:39
  108.3 0.0 copy-start.3
  108.3 0.0 reduce-scatter.2.cloned.1.call-update
  108.3 0.6 copy-done.3
  109.0 0.0 copy-done
  109.0 1.6 gather_fusion
  110.6 0.0 copy-start.2
  110.6 2.4 convert_select_fusion
  113.0 0.0 copy-done.2
  113.0 0.1 copy.16
  113.1 133.3 %all-reduce.1 = bf16[256,3072]{1,0:T(8,128)(2,1)S(1)} all-reduce(f32[256,3072]{1,0:T(8,128)} %convert_select_fusion), channel_id=1, replica_groups=mesh['row'=32,'col'=8] {'row','col'}, use_global_device_ids=true, to_apply=%region_0.1 | all-reduce | flops 786432 | bytes 4718592 | tf_op jit(solution)/shard_map/psum | solution.py:57
  246.4 0.6 fusion.18
  247.0 0.8 copy.19
  247.7 0.0 reduce-scatter.2.cloned.1.call-done
  (25 shorter events, 0.2 us)
Async XLA Ops:
  7.2 101.8 %copy-start = (bf16[128,3072]{1,0:T(8,128)(2,1)S(1)}, bf16[128,3072]{1,0:T(8,128)(2,1)}, u32[]{:S(2)}) copy-start(bf16[128,3072]{1,0:T(8,128)(2,1)} %param.12) | copy-start | bytes 2359300
  7.2 14.2 %copy-start.1 = (bf16[800,120]{1,0:T(8,128)(2,1)S(1)}, bf16[800,120]{1,0:T(8,128)(2,1)}, u32[]{:S(2)}) copy-start(bf16[800,120]{1,0:T(8,128)(2,1)} %param.15) | copy-start | bytes 576004
  8.9 43.8 %all-to-all-start = ((bf16[128,32,8]{0,2,1:T(8,128)(2,1)}), bf16[128,32,8]{0,2,1:T(8,128)(2,1)S(1)}, u32[]{:S(2)}, u32[]{:S(2)}) async-start(bf16[128,32,8]{0,2,1:T(8,128)(2,1)} %bitcast.4), calls=%async_computation | async-start | bytes 131072 | tf_op jit(solution)/shard_map/all_to_all | solution.py:64
  19.3 228.5 %reduce-scatter.2.cloned.1.call-start = ((), (), s32[]{:S(2)}) async-start(), calls=%async_computation.2 | async-start | bytes 3686400 | tf_op jit(solution)/shard_map/reduce_scatter | solution.py:68
  108.3 0.7 copy-start.3
  110.6 2.4 copy-start.2
Sparse Core Ops, SparseCore 0:
  108.4 78.8 reduce-scatter.1
where the time goes:
time: 255 us
  blocking collectives  133 us (52%)
  matrix products  51.2 us (20%)
  local copies, waits for them, and re-layouts  32.1 us (13%)
  between operations  14.2 us (6%)
  other arithmetic  13.1 us (5%)
  starting transfers between devices  10.5 us (4%)
    psum x1, blocking collectives, per_device(): pivot_rows = lax.psum(contribution, ('row', 'col')).astype(jnp.bfloat16)  133 us
    dot_general x8, matrix products, one_block(): jnp.einsum('pi,vpm->vim', coeff_block, spread, preferred_element_type=jnp...  50.6 us
    gather x1, local copies, waits for them, and re-layouts, half_transform(): jnp.take(occupied, second_ao, axis=0)  12.1 us
    gather x1, local copies, waits for them, and re-layouts, half_transform(): occ_first = jnp.take(occupied, first_ao, axis=0)  12.1 us
    all_to_all x1, starting transfers between devices, per_device(): lax.all_to_all(grouped, 'row', split_axis=1, concat_axis=0, tiled=True)  10.4 us
    unnamed x12, local copies, waits for them, and re-layouts  6.15 us
  transfers between devices with their start and end apart: 2, of which 0 were waited for; matrix products, arithmetic and copies ran while one was open for 15% of the time, Pallas kernels for 0%

commit v1 on v0

--- a/solution.py
+++ b/solution.py
@@ -2,6 +2,12 @@
 import jax.numpy as jnp
 from jax import lax
 from jax.sharding import PartitionSpec as P
+
+
+def treat_node(block_in, axis_key, axis_name):
+    for nth in (axis_key, axis_name):
+        block_in = lax.psum(block_in, nth)
+    return block_in
 
 
 def half_transform(received, pair_ids, occupied):
@@ -54,7 +60,7 @@
     owned = owner == own_index
     picked = jnp.take(prior, local_rows, axis=0).astype(jnp.float32)
     contribution = jnp.where(owned[:, None], picked, jnp.zeros_like(picked))
-    pivot_rows = lax.psum(contribution, ("row", "col")).astype(jnp.bfloat16)
+    pivot_rows = treat_node(contribution, "row", "col").astype(jnp.bfloat16)
     updated = panel - lax.dot_general(
         prior, pivot_rows, (((1,), (1,)), ((), ())), preferred_element_type=jnp.float32
     )

time: 255 us -> 497 us (1.95)
  waiting for transfers between devices: 0.02 us -> 249 us
  blocking collectives: 133 us -> 124 us
    psum x0 -> x1, waiting for transfers between devices: none -> 248 us  [treat_node(): block_in = lax.psum(block_in, nth)]
    psum x1, blocking collectives: 133 us -> 124 us  [treat_node(): block_in = lax.psum(block_in, nth)]
  transfers between devices with their start and end apart: 2 -> 3, of which waited for: 0 -> 1; matrix products, arithmetic and copies ran while one was open for 15% -> 19% of each run, Pallas kernels for 0% -> 0%
where the time goes in v1:
time: 497 us
  waiting for transfers between devices  249 us (50%)
  blocking collectives  124 us (25%)
  matrix products  51.5 us (10%)
  local copies, waits for them, and re-layouts  32.2 us (6%)
  between operations  15.7 us (3%)
  other arithmetic  13.9 us (3%)
  starting transfers between devices  10.5 us (2%)
    psum x1, waiting for transfers between devices, treat_node(): block_in = lax.psum(block_in, nth)  248 us
    psum x1, blocking collectives, treat_node(): block_in = lax.psum(block_in, nth)  124 us
    dot_general x8, matrix products, one_block(): jnp.einsum('pi,vpm->vim', coeff_block, spread, preferred_element_type=jnp...  50.9 us
    gather x1, local copies, waits for them, and re-layouts, half_transform(): jnp.take(occupied, second_ao, axis=0)  12.1 us
    gather x1, local copies, waits for them, and re-layouts, half_transform(): occ_first = jnp.take(occupied, first_ao, axis=0)  12.1 us
    all_to_all x1, starting transfers between devices, per_device(): lax.all_to_all(grouped, 'row', split_axis=1, concat_axis=0, tiled=True)  10.4 us
  transfers between devices with their start and end apart: 3, of which 1 were waited for; matrix products, arithmetic and copies ran while one was open for 19% of the time, Pallas kernels for 0%

profile of v1, /device:TPU:32, one launch (start us, length us, event | category | flops | bytes accessed | tf_op | source)
XLA Modules:
  0.0 496.7 jit_solution(16590286378519993348)
XLA Ops:
  8.0 0.0 copy-start
  8.0 1.6 copy.17
  9.7 10.4 %all-to-all-start = ((bf16[128,32,8]{0,2,1:T(8,128)(2,1)}), bf16[128,32,8]{0,2,1:T(8,128)(2,1)S(1)}, u32[]{:S(2)}, u32[]{:S(2)}) async-start(bf16[128,32,8]{0,2,1:T(8,128)(2,1)} %bitcast.4), calls=%async_computation | async-start | bytes 131072 | tf_op jit(solution)/shard_map/all_to_all | solution.py:70
  20.1 0.0 all-reduce.3.cloned.1.call-start
  20.1 0.7 compare_and_fusion.2
  20.8 0.0 copy-done
  20.9 1.6 gather_fusion
  22.4 0.0 copy-start.1
  22.4 2.4 convert_select_fusion
  24.9 0.0 all-reduce.3.cloned.1.call-update
  24.9 0.0 reduce-scatter.2.cloned.1.call-start
  24.9 1.0 broadcast_remainder_fusion
  25.9 1.0 compare_reduce_fusion
  27.0 0.0 copy-done.1
  27.0 12.1 %gather_fusion.2 = bf16[4096,120]{1,0:T(8,128)(2,1)S(1)} fusion(bf16[800,120]{1,0:T(8,128)(2,1)S(1)} %copy-done.1, s32[4096]{0:T(1024)S(1)} %get-tuple-element.172), kind=kCustom, calls=%fused_computation.1.clone | custom fusion | bytes 1982464 | tf_op jit(solution)/shard_map/jit(_take)/gather | solution.py:22
  39.1 12.1 %gather_fusion.1 = bf16[4096,120]{1,0:T(8,128)(2,1)S(1)} fusion(bf16[800,120]{1,0:T(8,128)(2,1)S(1)} %copy-done.1, s32[4096]{0:T(1024)S(1)} %fusion.21), kind=kCustom, calls=%fused_computation.clone | custom fusion | bytes 1982464 | tf_op jit(solution)/shard_map/jit(_take)/gather | solution.py:20
  51.3 2.1 broadcast_select_fusion
  53.4 1.4 select_select_fusion
  54.9 0.4 pad_maximum_fusion
  55.3 2.9 copy.18
  58.2 0.0 all-to-all-done
  58.2 55.9 %while.14 = (s32[]{:T(128)}, f32[8,120,800]{1,2,0:T(8,128)}, s32[8192]{0:T(1024)S(1)}, bf16[8192,8]{0,1:T(8,128)(2,1)S(1)}, bf16[8192,120]{0,1:T(8,128)(2,1)}, /*index=5*/s32[]{:T(128)}, s32[]{:T(128)}, s32[]{:T(128)}, s32[]{:T(128)}) while((s32[]{:T(128)}, f32[8,120,800]{1,2,0:T(8,128)}, s32[8192]{0:T(1024)S(1)}, ...), condition=%wide.region_3.5_spmd.clone, body=%wide.region_2.4_spmd.clone.sunk | while | flops 1581772800 | bytes 8294561 | solution.py:50
  58.2 0.6 iota_compare_fusion.2
  58.9 5.9 %bitcast_add_fusion.2 = f32[8,120,800]{1,2,0:T(8,128)} fusion(f32[8,120,800]{1,2,0:T(8,128)} %get-tuple-element.216, pred[1024,800]{0,1:T(8,128)(4,1)S(1)} %iota_compare_fusion.2, bf16[8,1024]{1,0:T(8,128)(2,1)S(1)} %dynamic-slice_bitcast_fusion.2, pred[]{:T(512)S(6)} %compare.6, bf16[8192,120]{0,1:T(8,128)(2,1)} %get-tuple-element.228, ...), kind=kOutput, calls=%fused_computation.9.clone.1 | convolution fusion | flops 1580953600 | bytes 7430149 | tf_op jit(solution)/shard_map/while/body/eval_jaxpr/pi,vpm->vim/dot_general | solution.py:45
  64.8 0.6 iota_compare_fusion.2
  65.4 6.4 %bitcast_add_fusion.2 = f32[8,120,800]{1,2,0:T(8,128)} fusion(f32[8,120,800]{1,2,0:T(8,128)} %get-tuple-element.216, pred[1024,800]{0,1:T(8,128)(4,1)S(1)} %iota_compare_fusion.2, bf16[8,1024]{1,0:T(8,128)(2,1)S(1)} %dynamic-slice_bitcast_fusion.2, pred[]{:T(512)S(6)} %compare.6, bf16[8192,120]{0,1:T(8,128)(2,1)} %get-tuple-element.228, ...), kind=kOutput, calls=%fused_computation.9.clone.1 | convolution fusion | flops 1580953600 | bytes 7430149 | tf_op jit(solution)/shard_map/while/body/eval_jaxpr/pi,vpm->vim/dot_general | solution.py:45
  71.9 0.6 iota_compare_fusion.2
  72.5 6.4 %bitcast_add_fusion.2 = f32[8,120,800]{1,2,0:T(8,128)} fusion(f32[8,120,800]{1,2,0:T(8,128)} %get-tuple-element.216, pred[1024,800]{0,1:T(8,128)(4,1)S(1)} %iota_compare_fusion.2, bf16[8,1024]{1,0:T(8,128)(2,1)S(1)} %dynamic-slice_bitcast_fusion.2, pred[]{:T(512)S(6)} %compare.6, bf16[8192,120]{0,1:T(8,128)(2,1)} %get-tuple-element.228, ...), kind=kOutput, calls=%fused_computation.9.clone.1 | convolution fusion | flops 1580953600 | bytes 7430149 | tf_op jit(solution)/shard_map/while/body/eval_jaxpr/pi,vpm->vim/dot_general | solution.py:45
  78.9 0.6 iota_compare_fusion.2
  79.5 6.4 %bitcast_add_fusion.2 = f32[8,120,800]{1,2,0:T(8,128)} fusion(f32[8,120,800]{1,2,0:T(8,128)} %get-tuple-element.216, pred[1024,800]{0,1:T(8,128)(4,1)S(1)} %iota_compare_fusion.2, bf16[8,1024]{1,0:T(8,128)(2,1)S(1)} %dynamic-slice_bitcast_fusion.2, pred[]{:T(512)S(6)} %compare.6, bf16[8192,120]{0,1:T(8,128)(2,1)} %get-tuple-element.228, ...), kind=kOutput, calls=%fused_computation.9.clone.1 | convolution fusion | flops 1580953600 | bytes 7430149 | tf_op jit(solution)/shard_map/while/body/eval_jaxpr/pi,vpm->vim/dot_general | solution.py:45
  86.0 0.6 iota_compare_fusion.2
  86.6 6.4 %bitcast_add_fusion.2 = f32[8,120,800]{1,2,0:T(8,128)} fusion(f32[8,120,800]{1,2,0:T(8,128)} %get-tuple-element.216, pred[1024,800]{0,1:T(8,128)(4,1)S(1)} %iota_compare_fusion.2, bf16[8,1024]{1,0:T(8,128)(2,1)S(1)} %dynamic-slice_bitcast_fusion.2, pred[]{:T(512)S(6)} %compare.6, bf16[8192,120]{0,1:T(8,128)(2,1)} %get-tuple-element.228, ...), kind=kOutput, calls=%fused_computation.9.clone.1 | convolution fusion | flops 1580953600 | bytes 7430149 | tf_op jit(solution)/shard_map/while/body/eval_jaxpr/pi,vpm->vim/dot_general | solution.py:45
  93.0 0.6 iota_compare_fusion.2
  93.6 6.4 %bitcast_add_fusion.2 = f32[8,120,800]{1,2,0:T(8,128)} fusion(f32[8,120,800]{1,2,0:T(8,128)} %get-tuple-element.216, pred[1024,800]{0,1:T(8,128)(4,1)S(1)} %iota_compare_fusion.2, bf16[8,1024]{1,0:T(8,128)(2,1)S(1)} %dynamic-slice_bitcast_fusion.2, pred[]{:T(512)S(6)} %compare.6, bf16[8192,120]{0,1:T(8,128)(2,1)} %get-tuple-element.228, ...), kind=kOutput, calls=%fused_computation.9.clone.1 | convolution fusion | flops 1580953600 | bytes 7430149 | tf_op jit(solution)/shard_map/while/body/eval_jaxpr/pi,vpm->vim/dot_general | solution.py:45
  100.0 0.6 iota_compare_fusion.2
  100.7 6.4 %bitcast_add_fusion.2 = f32[8,120,800]{1,2,0:T(8,128)} fusion(f32[8,120,800]{1,2,0:T(8,128)} %get-tuple-element.216, pred[1024,800]{0,1:T(8,128)(4,1)S(1)} %iota_compare_fusion.2, bf16[8,1024]{1,0:T(8,128)(2,1)S(1)} %dynamic-slice_bitcast_fusion.2, pred[]{:T(512)S(6)} %compare.6, bf16[8192,120]{0,1:T(8,128)(2,1)} %get-tuple-element.228, ...), kind=kOutput, calls=%fused_computation.9.clone.1 | convolution fusion | flops 1580953600 | bytes 7430149 | tf_op jit(solution)/shard_map/while/body/eval_jaxpr/pi,vpm->vim/dot_general | solution.py:45
  107.1 0.6 iota_compare_fusion.2
  107.7 6.4 %bitcast_add_fusion.2 = f32[8,120,800]{1,2,0:T(8,128)} fusion(f32[8,120,800]{1,2,0:T(8,128)} %get-tuple-element.216, pred[1024,800]{0,1:T(8,128)(4,1)S(1)} %iota_compare_fusion.2, bf16[8,1024]{1,0:T(8,128)(2,1)S(1)} %dynamic-slice_bitcast_fusion.2, pred[]{:T(512)S(6)} %compare.6, bf16[8192,120]{0,1:T(8,128)(2,1)} %get-tuple-element.228, ...), kind=kOutput, calls=%fused_computation.9.clone.1 | convolution fusion | flops 1580953600 | bytes 7430149 | tf_op jit(solution)/shard_map/while/body/eval_jaxpr/pi,vpm->vim/dot_general | solution.py:45
  114.1 0.0 copy-start.2
  114.1 0.0 reduce-scatter.2.cloned.1.call-update
  114.2 0.9 copy-done.2
  115.0 0.1 copy.16
  115.1 248.5 %all-reduce.3.cloned.1.call-done = f32[256,3072]{1,0:T(8,128)} async-done(((f32[256,3072]{1,0:T(8,128)}), f32[256,3072]{1,0:T(8,128)}) %all-reduce.3.cloned.1.call-update) | async-done | bytes 3145744 | tf_op jit(solution)/shard_map/psum | solution.py:9
  363.6 124.2 %all-reduce.4 = bf16[256,3072]{1,0:T(8,128)(2,1)S(1)} all-reduce(f32[256,3072]{1,0:T(8,128)} %all-reduce.3.cloned.1.call-done), channel_id=1, replica_groups=mesh['row'=32,'col'=8] {'col'}, use_global_device_ids=true, to_apply=%region_1.2 | all-reduce | flops 786432 | bytes 4718592 | tf_op jit(solution)/shard_map/psum | solution.py:9
  487.9 0.6 fusion.18
  488.4 0.8 copy.19
  489.2 0.0 reduce-scatter.2.cloned.1.call-done
  (24 shorter events, 0.2 us)
Async XLA Ops:
  8.0 12.9 %copy-start = (bf16[128,3072]{1,0:T(8,128)(2,1)S(1)}, bf16[128,3072]{1,0:T(8,128)(2,1)}, u32[]{:S(2)}) copy-start(bf16[128,3072]{1,0:T(8,128)(2,1)} %param.12) | copy-start | bytes 2359300
  9.7 48.5 %all-to-all-start = ((bf16[128,32,8]{0,2,1:T(8,128)(2,1)}), bf16[128,32,8]{0,2,1:T(8,128)(2,1)S(1)}, u32[]{:S(2)}, u32[]{:S(2)}) async-start(bf16[128,32,8]{0,2,1:T(8,128)(2,1)} %bitcast.4), calls=%async_computation | async-start | bytes 131072 | tf_op jit(solution)/shard_map/all_to_all | solution.py:70
  20.1 343.6 %all-reduce.3.cloned.1.call-start = ((), (), s32[]{:S(2)}) async-start(), calls=%async_computation.2 | async-start | bytes 6291456 | tf_op jit(solution)/shard_map/psum | solution.py:9
  22.4 4.6 copy-start.1
  24.9 464.3 %reduce-scatter.2.cloned.1.call-start = ((), (), s32[]{:S(2)}) async-start(), calls=%async_computation.3 | async-start | bytes 3686400 | tf_op jit(solution)/shard_map/reduce_scatter | solution.py:74
  114.1 0.9 copy-start.2
Sparse Core Ops, SparseCore 0:
  25.0 338.5 all-reduce.2
Sparse Core Ops, SparseCore 1:
  114.3 83.2 reduce-scatter.1
